TPU v7x, 1024 devices: a whole 8x8x8 slice. The times are simulated.
1024 devices in a mesh: prow: 16 (over y, core), pcol: 64 (over x, z).
Axes of the slice: x: 8, y: 8, z: 8, core: 2. Of those that a mesh axis runs over, the one named last changes fastest.
Arguments:
- slab: bfloat16 [32768, 24576], P('prow', 'pcol'), may hold values from -6 to 6
- pivots: int32 [512], replicated, may hold values from 0 to 32767, as said below
- l_top: bfloat16 [512, 512], replicated, may hold values from -0.125 to 0.125
- l_panel_t: bfloat16 [512, 32768], P('pcol', 'prow'), may hold values from -0.125 to 0.125
Outputs:
- result: bfloat16 [32768, 24576], P('prow', 'pcol')
Inputs may be any that keep to these rules, and one draw needn't show every extreme that they name: `pivots`: distinct rows; how many fall on each index of prow is uneven and changes with the draw.
All inputs are finite; a program needn't handle non-finite values.
Results may differ from a plain program's by a relative error of at most 0.0029.
Values may be sent and summed in bfloat16 or wider, within the bound.
No kernel may reach another device: no remote copies, remote signals or barrier semaphores. Data moves between devices by JAX's collectives and lax.ppermute only.
A program may use at most 64 MiB of HBM per device.

v0:
```python
import jax
import jax.numpy as jnp
from jax import lax
from jax.experimental import pallas as pl
from jax.experimental.pallas import tpu as pltpu
from jax.sharding import PartitionSpec as P


BF, F32 = jnp.bfloat16, jnp.float32
HI = lax.Precision.HIGHEST


CAP = 80
ROOM = pltpu.CompilerParams(vmem_limit_bytes=20 * 2**20)


def column(row):
    n = row.shape[1]
    eye = lax.broadcasted_iota(jnp.int32, (n, n), 0) == lax.broadcasted_iota(jnp.int32, (n, n), 1)
    return jnp.sum(jnp.where(eye, row, 0.0), axis=1, keepdims=True)


def pick_kernel(where_ref, pivot_ref, slab_ref, pick_ref, place_ref, dest_ref, most_ref):
    n, rows = pivot_ref.shape[1], slab_ref.shape[0]
    me, base = where_ref[0], where_ref[1].astype(F32)
    p_int = pivot_ref[...]
    p_row = p_int.astype(F32)
    p_col = column(p_row)
    o_row = (p_int // rows).astype(F32)
    o_col = column(o_row)
    sub = lax.broadcasted_iota(jnp.int32, (n, n), 0)
    lane = lax.broadcasted_iota(jnp.int32, (n, n), 1)
    same = o_col == o_row
    rank_row = jnp.sum(jnp.where(same & (sub < lane), 1.0, 0.0), axis=0, keepdims=True)
    rank_col = jnp.sum(jnp.where(same & (lane < sub), 1.0, 0.0), axis=1, keepdims=True)
    most_ref[0] = jnp.max(rank_row).astype(jnp.int32) + 1
    slot = rank_col - base
    place_ref[...] = jnp.where((slot >= 0) & (slot < CAP), o_col * CAP + slot, -1.0).astype(jnp.int32)

    index = lax.broadcasted_iota(jnp.int32, (CAP, n), 0).astype(F32) + base
    chosen = (o_row == me.astype(F32)) & (rank_row == index)
    local = jnp.sum(jnp.where(chosen, p_row - (me * rows).astype(F32), 0.0), axis=1, keepdims=True)
    hot = lax.broadcasted_iota(jnp.int32, (CAP, rows), 1) == local.astype(jnp.int32)
    pick_ref[...] = jnp.dot(hot.astype(BF), slab_ref[...], preferred_element_type=F32).astype(BF)

    taken = jnp.where(p_col == lane.astype(F32), 1.0, 0.0)
    free_row = 1.0 - jnp.max(taken, axis=0, keepdims=True)
    free_col = column(free_row)
    far_row = jnp.where(p_row >= n, 1.0, 0.0)
    far_col = jnp.where(p_col >= n, 1.0, 0.0)
    free_rank = jnp.sum(jnp.where(sub < lane, free_col, 0.0), axis=0, keepdims=True)
    far_rank = jnp.sum(jnp.where(lane < sub, far_row, 0.0), axis=1, keepdims=True)
    match = (far_rank == free_rank) & (far_col > 0) & (free_row > 0)
    dest_ref[...] = (jnp.sum(jnp.where(match, p_col + 1.0, 0.0), axis=0, keepdims=True) - 1.0).astype(jnp.int32)


def pick(where, pivots, slab):
    n, w = pivots.shape[0], slab.shape[1]
    vmem = pl.BlockSpec(memory_space=pltpu.VMEM)
    return pl.pallas_call(
        pick_kernel,
        in_specs=[pl.BlockSpec(memory_space=pltpu.SMEM), vmem, vmem],
        out_shape=[
            jax.ShapeDtypeStruct((CAP, w), BF),
            jax.ShapeDtypeStruct((n, 1), jnp.int32),
            jax.ShapeDtypeStruct((1, n), jnp.int32),
            jax.ShapeDtypeStruct((1,), jnp.int32),
        ],
        out_specs=[vmem, vmem, vmem, pl.BlockSpec(memory_space=pltpu.SMEM)],
        compiler_params=ROOM,
        cost_estimate=pl.CostEstimate(flops=2 * 10**9, bytes_accessed=2 * slab.size, transcendentals=0),
    )(where, pivots[None], slab)


def mm(a, b):
    return jnp.dot(a, b, precision=HI, preferred_element_type=F32)


def inverse_kernel(l_ref, a_ref, b_ref, x_ref):
    n, t = l_ref.shape[0], 128
    row = lax.broadcasted_iota(jnp.int32, (t, t), 0)
    col = lax.broadcasted_iota(jnp.int32, (t, t), 1)
    eye = (row == col).astype(F32)
    x_ref[...] = jnp.zeros_like(x_ref)
    blocks = range(n // t)
    low = [
        jnp.where(row > col, l_ref[b * t : (b + 1) * t, b * t : (b + 1) * t].astype(F32), 0.0)
        for b in blocks
    ]
    step = 16
    near = [jnp.where(row // step == col // step, v, 0.0) for v in low]
    inv = [eye - v for v in near]
    power = near
    for _ in range(3):
        power = [mm(v, v) for v in power]
        inv = [x + mm(x, v) for x, v in zip(inv, power)]
    while step < t:
        off = [
            jnp.where((row // (2 * step) == col // (2 * step)) & (row // step != col // step), v, 0.0)
            for v in low
        ]
        half = [mm(x, v) for x, v in zip(inv, off)]
        inv = [x - mm(h, x) for x, h in zip(inv, half)]
        step *= 2
    for b in blocks:
        x_ref[b * t : (b + 1) * t, b * t : (b + 1) * t] = inv[b]
    size = t
    while size < n:
        for s in range(0, n, 2 * size):
            top, bot = slice(s, s + size), slice(s + size, s + 2 * size)
            x_ref[bot, top] = -mm(x_ref[bot, bot], mm(l_ref[bot, top].astype(F32), x_ref[top, top]))
        size *= 2
    x = x_ref[...]
    a = x.astype(BF)
    a_ref[...] = a
    b_ref[...] = (x - a.astype(F32)).astype(BF)


def inverse(l_top):
    n = l_top.shape[0]
    shape = jax.ShapeDtypeStruct((n, n), BF)
    return pl.pallas_call(
        inverse_kernel,
        out_shape=[shape] * 2,
        scratch_shapes=[pltpu.VMEM((n, n), F32)],
        compiler_params=ROOM,
        cost_estimate=pl.CostEstimate(flops=2 * 10**9, bytes_accessed=4 * n * n * 2, transcendentals=0),
    )(l_top)


def placed(place_ref, got_ref):
    hot = lax.broadcasted_iota(jnp.int32, (place_ref.shape[0], got_ref.shape[0]), 1) == place_ref[...]
    return jnp.dot(hot.astype(BF), got_ref[...], preferred_element_type=F32)


def finish(row_ref, a_ref, b_ref, top, u_ref, v_ref):
    u = jnp.dot(b_ref[...], top, preferred_element_type=F32)
    u += jnp.dot(a_ref[...], top, preferred_element_type=F32)
    u_ref[...] = u.astype(BF)
    for core in range(2):
        @pl.when(row_ref[0] % 2 == core)
        def _():
            order = [column_of(core, *b, *p) * 8 for p in NEXT for b in FAR]
            v_ref[...] = (-jnp.concatenate([u[i : i + 8] for i in order], axis=0)).astype(BF)


def place_solve_kernel(row_ref, a_ref, b_ref, place_ref, got_ref, u_ref, v_ref):
    finish(row_ref, a_ref, b_ref, placed(place_ref, got_ref).astype(BF), u_ref, v_ref)


def solve_kernel(row_ref, a_ref, b_ref, top_ref, u_ref, v_ref):
    finish(row_ref, a_ref, b_ref, top_ref[...], u_ref, v_ref)


def add_kernel(top_ref, place_ref, got_ref, out_ref):
    out_ref[...] = (top_ref[...].astype(F32) + placed(place_ref, got_ref)).astype(BF)


def solve(kernel, row, parts, *rest):
    n, w = parts[0].shape[0], rest[-1].shape[1]
    shape = jax.ShapeDtypeStruct((n, w), BF)
    vmem = pl.BlockSpec(memory_space=pltpu.VMEM)
    return tuple(pl.pallas_call(
        kernel,
        in_specs=[pl.BlockSpec(memory_space=pltpu.SMEM)] + [vmem] * (2 + len(rest)),
        out_shape=[shape] * 2,
        compiler_params=ROOM,
        cost_estimate=pl.CostEstimate(flops=10**9, bytes_accessed=10**7, transcendentals=0),
    )(row, *parts, *rest))


def update_kernel(row_ref, l_ref, u_ref, v_ref, dest_ref, own_ref, sent_ref, slab_ref, out_ref, right_ref):
    j = pl.program_id(0)
    rows, w = slab_ref.shape
    n = u_ref.shape[0]

    @pl.when(j == 0)
    def _():
        right_ref[:n, :w] = v_ref[...]
        right_ref[:n, w:] = jnp.zeros_like(right_ref[:n, w:])
        right_ref[n:, w:] = jnp.ones_like(right_ref[n:, w:])

        @pl.when(row_ref[0] % 2 == 0)
        def _():
            right_ref[n:, :w] = own_ref[...]

        @pl.when(row_ref[0] % 2 == 1)
        def _():
            right_ref[n:, :w] = sent_ref[...]

    first = (row_ref[0] * pl.num_programs(0) + j) * rows
    hit = first + lax.broadcasted_iota(jnp.int32, (rows, n), 0) == dest_ref[...]
    left = jnp.concatenate([l_ref[...].T, hit.astype(BF)], axis=1)
    acc = jnp.dot(left, right_ref[...], preferred_element_type=F32)
    lost = jnp.concatenate([acc[:, w:]] * (w // 128), axis=1)
    out_ref[...] = (jnp.where(lost > 0, 0.0, slab_ref[...].astype(F32)) + acc[:, :w]).astype(BF)

    @pl.when((row_ref[0] == 0) & (j == 0))
    def _():
        out_ref[:n, :] = u_ref[...]


def by_rows(kernel, rows, out, args, flops, scratch):
    specs = [pl.BlockSpec(memory_space=pltpu.SMEM)]
    for a in args[1:]:
        if not isinstance(a, tuple):
            specs.append(pl.BlockSpec(a.shape, lambda j: (0, 0)))
        elif a[1] == 0:
            specs.append(pl.BlockSpec((rows, a[0].shape[1]), lambda j: (j, 0)))
        else:
            specs.append(pl.BlockSpec((a[0].shape[0], rows), lambda j: (0, j)))
    arrays = [a[0] if isinstance(a, tuple) else a for a in args]
    return pl.pallas_call(
        kernel,
        grid=(out[0] // rows,),
        in_specs=specs,
        out_specs=pl.BlockSpec((rows, out[1]), lambda j: (j, 0)),
        out_shape=jax.ShapeDtypeStruct(out, BF),
        scratch_shapes=scratch,
        compiler_params=ROOM,
        cost_estimate=pl.CostEstimate(flops=flops, bytes_accessed=6 * 2**20, transcendentals=0),
    )(*arrays)


def chip(row, block, place):
    return (2 * block + place + row % 2) % 8


def column_of(row, bx, bz, px, pz):
    return chip(row, bx, px) * 8 + chip(row, bz, pz)


FAR = [(bx, bz) for bx in range(4) for bz in range(4)]
NEXT = [(px, pz) for px in range(2) for pz in range(2)]


def far_groups():
    return [[row * 64 + column_of(row, *b, *p) for b in FAR] for row in range(16) for p in NEXT]


def next_groups():
    return [[row * 64 + column_of(row, *b, *p) for p in NEXT] for row in range(16) for b in FAR]


def exchange(block, groups):
    copies = jnp.broadcast_to(block[None], (len(groups[0]),) + block.shape)
    return lax.all_to_all(copies, ("prow", "pcol"), 0, 0, axis_index_groups=groups)


def hand_on(home, size):
    return lax.ppermute(home, "prow", [(i, i + size // 2) for i in range(0, 16, size)])


def step_of_panel(slab, pivots, l_top, l_panel_t):
    local_rows, w = slab.shape
    n = pivots.shape[0]
    k = l_panel_t.shape[0]
    row = lax.axis_index("prow").astype(jnp.int32)
    r = row.reshape(1)

    def picks(base):
        return pick(jnp.stack([row, base]), pivots, slab)

    near = exchange(l_panel_t, far_groups()).reshape(16 * k, local_rows)
    home = slab[:n]
    got = hand_on(home, 16)
    got, l_top = lax.optimization_barrier((got, l_top))
    home = jnp.where(row == 0, home, got)
    got = hand_on(home, 8)
    parts = inverse(l_top)
    picked, place, dest, most = picks(jnp.int32(0))
    near, got, picked, parts = lax.optimization_barrier((near, got, picked, parts))
    home = jnp.where(row % 8 == 0, home, got)
    got = hand_on(home, 4)
    panel = exchange(near, next_groups()).reshape(n, local_rows)
    rows = lax.all_gather(picked, "prow", axis=0, tiled=True)
    got, rows = lax.optimization_barrier((got, rows))
    home = jnp.where(row % 4 == 0, home, got)
    sent = hand_on(home, 2)
    u, v = solve(place_solve_kernel, r, parts, place, rows)

    def in_rounds(_):
        def step(state):
            base, top = state
            picked, place, _, _ = picks(base)
            rows = lax.all_gather(picked, "prow", axis=0, tiled=True)
            top = pl.pallas_call(add_kernel, out_shape=jax.ShapeDtypeStruct((n, w), BF))(top, place, rows)
            return base + CAP, top

        _, top = lax.while_loop(lambda s: s[0] < most[0], step, (jnp.int32(0), jnp.zeros((n, w), BF)))
        return False, *solve(solve_kernel, r, parts, top)

    _, u, v = lax.while_loop(lambda s: s[0], in_rounds, (most[0] > CAP, u, v))
    flops = 4 * local_rows * n * w
    args = (r, (panel, 1), u, v, dest, home, sent, (slab, 0))
    return by_rows(update_kernel, 512, slab.shape, args, flops, [pltpu.VMEM((2 * n, w + 128), BF)])


def solution(mesh):
    return jax.shard_map(
        step_of_panel,
        mesh=mesh,
        in_specs=(P("prow", "pcol"), P(), P(), P("pcol", "prow")),
        out_specs=P("prow", "pcol"),
        check_vma=False,
    )
```

profile of v0, /device:TPU:1, one launch (start us, length us, event | category | flops | bytes accessed | tf_op | source)
XLA Modules:
  0.0 84.6 jit_solution(9256733426448189011)
XLA Ops:
  0.0 0.0 copy-start.2
  0.0 1.2 %slice.3 = bf16[512,384]{1,0:T(8,128)(2,1)S(1)} slice(bf16[2048,384]{1,0:T(8,128)(2,1)} %slab_ref.3), slice={[0:512], [0:384]} | slice | bytes 786432 | tf_op jit(solution)/shard_map/slice | solution.py:265
  1.2 0.0 copy-start.3
  1.2 0.7 collective-permute-start
  1.9 1.6 %broadcast_in_dim.8 = bf16[16,8,2048]{2,1,0:T(8,128)(2,1)} broadcast(bf16[8,2048]{1,0:T(8,128)(2,1)} %param.11), dimensions={1,2} | broadcast | bytes 557056 | tf_op jit(solution)/shard_map/broadcast_in_dim | solution.py:246
  3.5 23.4 %all-to-all-start = ((bf16[16,8,2048]{2,1,0:T(8,128)(2,1)}), bf16[16,8,2048]{2,1,0:T(8,128)(2,1)}, u32[]{:S(2)}, u32[]{:S(2)}) async-start(bf16[16,8,2048]{2,1,0:T(8,128)(2,1)} %broadcast_in_dim.8), calls=%async_computation | async-start | bytes 1048576 | tf_op jit(solution)/shard_map/all_to_all | solution.py:247
  26.8 0.0 collective-permute-done
  26.9 0.0 copy-done.2
  26.9 0.1 broadcast_select_fusion.2
  26.9 0.7 collective-permute-start.1
  27.6 0.1 pad_add_fusion.1.where_ref
  27.7 0.0 copy-done.3
  27.7 0.0 copy-start.1
  27.7 1.9 %shard_map.46 = (bf16[80,384]{1,0:T(8,128)(2,1)S(1)}, s32[512,1]{1,0:T(8,128)S(1)}, s32[1,512]{1,0:T(1,128)S(1)}, s32[1]{0:T(128)}) custom-call(s32[2]{0:T(128)S(1)} %pad_add_fusion.1.where_ref, s32[1,512]{1,0:T(1,128)S(1)} %bitcast.17, bf16[2048,384]{1,0:T(8,128)(2,1)S(1)} %copy-done.2), custom_call_target="tpu_custom_call" | custom-call | flops 2000000000 | bytes 1572864 | tf_op jit(solution)/shard_map/pallas_call | solution.py:60
  30.2 0.0 copy-done.1
  30.2 5.3 %shard_map.47 = (bf16[512,512]{1,0:T(8,128)(2,1)}, bf16[512,512]{1,0:T(8,128)(2,1)}) custom-call(bf16[512,512]{1,0:T(8,128)(2,1)S(1)} %copy-done.1), custom_call_target="tpu_custom_call" | custom-call | flops 2000000000 | bytes 2097152 | tf_op jit(solution)/shard_map/pallas_call | solution.py:122
  35.5 0.0 collective-permute-done.1
  35.5 4.2 %all-to-all-done = bf16[16,8,2048]{2,1,0:T(8,128)(2,1)} async-done(((bf16[16,8,2048]{2,1,0:T(8,128)(2,1)}), bf16[16,8,2048]{2,1,0:T(8,128)(2,1)}, u32[]{:S(2)}, u32[]{:S(2)}) %all-to-all-start) | async-done | bytes 524320 | tf_op jit(solution)/shard_map/all_to_all | solution.py:247
  39.8 0.7 collective-permute-start.2
  40.5 2.6 %broadcast_in_dim.20 = bf16[4,128,2048]{2,1,0:T(8,128)(2,1)} broadcast(bf16[128,2048]{1,0:T(8,128)(2,1)} %bitcast.5), dimensions={1,2} | broadcast | bytes 2621440 | tf_op jit(solution)/shard_map/broadcast_in_dim | solution.py:246
  43.1 6.1 %all-to-all-start.1 = ((bf16[4,128,2048]{2,1,0:T(8,128)(2,1)}), bf16[4,128,2048]{2,1,0:T(8,128)(2,1)S(1)}, u32[]{:S(2)}, u32[]{:S(2)}) async-start(bf16[4,128,2048]{2,1,0:T(8,128)(2,1)} %broadcast_in_dim.20), calls=%async_computation.1 | async-start | bytes 4194304 | tf_op jit(solution)/shard_map/all_to_all | solution.py:247
  49.2 0.0 copy-start.4
  49.2 0.0 copy-start.6
  49.2 26.0 %all_gather.6.got_ref = bf16[1280,384]{1,0:T(8,128)(2,1)S(1)} all-gather(bf16[80,384]{1,0:T(8,128)(2,1)S(1)} %get-tuple-element.120), channel_id=1, replica_groups=mesh['prow'=16,'pcol'=64] {'prow'}, dimensions={0}, use_global_device_ids=true | all-gather | bytes 1044480 | tf_op jit(solution)/shard_map/all_gather | solution.py:276
  75.2 0.0 collective-permute-done.2
  75.2 1.3 %collective-permute-start.3 = (bf16[512,384]{1,0:T(8,128)(2,1)S(1)}, bf16[512,384]{1,0:T(8,128)(2,1)S(1)}, u32[]{:S(2)}, u32[]{:S(2)}) collective-permute-start(bf16[512,384]{1,0:T(8,128)(2,1)S(1)} %broadcast_select_fusion.own_ref), channel_id=1, source_target_pairs={{0,64},{128,192},{256,320},{384,448},{512,576},{640,704},{768,832}... | collective-permute-start | bytes 1179656 | tf_op jit(solution)/shard_map/ppermute | solution.py:251
  76.5 0.0 copy-done.4
  76.5 0.0 copy-done.6
  76.6 2.5 %shard_map.48 = (bf16[512,384]{1,0:T(8,128)(2,1)}, bf16[512,384]{1,0:T(8,128)(2,1)}) custom-call(s32[1]{0:T(128)} %bitcast.4.row_ref, bf16[512,512]{1,0:T(8,128)(2,1)S(1)} %copy-done.4, bf16[512,512]{1,0:T(8,128)(2,1)S(1)} %copy-done.6, s32[512,1]{1,0:T(8,128)S(1)} %get-tuple-element.118.place_ref, bf16[1280,384]{1,0:T(8,128)(2,1)S(1)} %all_gather.6.got_ref), custom_call_target="tpu_custom_call" | custom-call | flops 1000000000 | bytes 10000000 | tf_op jit(solution)/shard_map/pallas_call | solution.py:163
  79.0 0.0 collective-permute-done.3.sent_ref
  79.0 0.0 all-to-all-done.1
  79.0 5.6 %shard_map.49 = bf16[2048,384]{1,0:T(8,128)(2,1)} custom-call(s32[1]{0:T(128)} %bitcast.4.row_ref, bf16[512,2048]{1,0:T(8,128)(2,1)S(1)} %bitcast.16, bf16[512,384]{1,0:T(8,128)(2,1)} %get-tuple-element.301, bf16[512,384]{1,0:T(8,128)(2,1)} %get-tuple-element.302, s32[1,512]{1,0:T(1,128)S(1)} %get-tuple-element.126.dest_ref, ...), custom_call_target="tpu_custom_call" | custom-call | flops 1610612736 | bytes 6291456 | tf_op jit(solution)/shard_map/pallas_call | solution.py:213
  (3 shorter events, 0.1 us)
Async XLA Ops:
  0.0 26.9 %copy-start.2 = (bf16[2048,384]{1,0:T(8,128)(2,1)S(1)}, bf16[2048,384]{1,0:T(8,128)(2,1)}, u32[]{:S(2)}) copy-start(bf16[2048,384]{1,0:T(8,128)(2,1)} %slab_ref.3) | copy-start | bytes 4718596
  1.2 26.5 %copy-start.3 = (s32[512]{0:T(512)S(1)}, s32[512]{0:T(512)}, u32[]{:S(2)}) copy-start(s32[512]{0:T(512)} %param.9) | copy-start | bytes 6148
  1.2 25.7 %collective-permute-start = (bf16[512,384]{1,0:T(8,128)(2,1)S(1)}, bf16[512,384]{1,0:T(8,128)(2,1)S(1)}, u32[]{:S(2)}, u32[]{:S(2)}) collective-permute-start(bf16[512,384]{1,0:T(8,128)(2,1)S(1)} %slice.3), channel_id=1, source_target_pairs={{0,512},{1,513},{2,514},{3,515},{4,516},{5,517},{6,518},{7,519},{8... | collective-permute-start | bytes 1179656 | tf_op jit(solution)/shard_map/ppermute | solution.py:251
  3.5 36.3 %all-to-all-start = ((bf16[16,8,2048]{2,1,0:T(8,128)(2,1)}), bf16[16,8,2048]{2,1,0:T(8,128)(2,1)}, u32[]{:S(2)}, u32[]{:S(2)}) async-start(bf16[16,8,2048]{2,1,0:T(8,128)(2,1)} %broadcast_in_dim.8), calls=%async_computation | async-start | bytes 1048576 | tf_op jit(solution)/shard_map/all_to_all | solution.py:247
  26.9 8.6 %collective-permute-start.1 = (bf16[512,384]{1,0:T(8,128)(2,1)S(1)}, bf16[512,384]{1,0:T(8,128)(2,1)S(1)}, u32[]{:S(2)}, u32[]{:S(2)}) collective-permute-start(bf16[512,384]{1,0:T(8,128)(2,1)S(1)} %broadcast_select_fusion.2), channel_id=1, source_target_pairs={{0,256},{512,768},{1,257},{513,769},{2,258},{514,770},{3,259},{515... | collective-permute-start | bytes 1179656 | tf_op jit(solution)/shard_map/ppermute | solution.py:251
  27.7 2.5 %copy-start.1 = (bf16[512,512]{1,0:T(8,128)(2,1)S(1)}, bf16[512,512]{1,0:T(8,128)(2,1)}, u32[]{:S(2)}) copy-start(bf16[512,512]{1,0:T(8,128)(2,1)} %l_ref) | copy-start | bytes 1572868
  39.8 35.4 %collective-permute-start.2 = (bf16[512,384]{1,0:T(8,128)(2,1)S(1)}, bf16[512,384]{1,0:T(8,128)(2,1)S(1)}, u32[]{:S(2)}, u32[]{:S(2)}) collective-permute-start(bf16[512,384]{1,0:T(8,128)(2,1)S(1)} %broadcast_select_fusion.1), channel_id=1, source_target_pairs={{0,128},{256,384},{512,640},{768,896},{1,129},{257,385},{513,641},... | collective-permute-start | bytes 1179656 | tf_op jit(solution)/shard_map/ppermute | solution.py:251
  43.1 35.9 %all-to-all-start.1 = ((bf16[4,128,2048]{2,1,0:T(8,128)(2,1)}), bf16[4,128,2048]{2,1,0:T(8,128)(2,1)S(1)}, u32[]{:S(2)}, u32[]{:S(2)}) async-start(bf16[4,128,2048]{2,1,0:T(8,128)(2,1)} %broadcast_in_dim.20), calls=%async_computation.1 | async-start | bytes 4194304 | tf_op jit(solution)/shard_map/all_to_all | solution.py:247
  49.2 27.4 %copy-start.4 = (bf16[512,512]{1,0:T(8,128)(2,1)S(1)}, bf16[512,512]{1,0:T(8,128)(2,1)}, u32[]{:S(2)}) copy-start(bf16[512,512]{1,0:T(8,128)(2,1)} %get-tuple-element.241.a_ref) | copy-start | bytes 1572868
  49.2 27.4 %copy-start.6 = (bf16[512,512]{1,0:T(8,128)(2,1)S(1)}, bf16[512,512]{1,0:T(8,128)(2,1)}, u32[]{:S(2)}) copy-start(bf16[512,512]{1,0:T(8,128)(2,1)} %get-tuple-element.242.b_ref) | copy-start | bytes 1572868
  75.2 3.8 %collective-permute-start.3 = (bf16[512,384]{1,0:T(8,128)(2,1)S(1)}, bf16[512,384]{1,0:T(8,128)(2,1)S(1)}, u32[]{:S(2)}, u32[]{:S(2)}) collective-permute-start(bf16[512,384]{1,0:T(8,128)(2,1)S(1)} %broadcast_select_fusion.own_ref), channel_id=1, source_target_pairs={{0,64},{128,192},{256,320},{384,448},{512,576},{640,704},{768,832}... | collective-permute-start | bytes 1179656 | tf_op jit(solution)/shard_map/ppermute | solution.py:251
where the time goes:
time: 85.6 us; the launch traced here: 84.6 us
  starting transfers between devices  32.8 us (38%)
  blocking collectives  26 us (30%)
  Pallas kernels  15.2 us (18%)
  local copies, waits for them, and re-layouts  5.41 us (6%)
  waiting for transfers between devices  4.23 us (5%)
    all_to_all x2, starting transfers between devices, exchange(): lax.all_to_all(copies, ('prow', 'pcol'), 0, 0, axis_index_groups=groups)  29.4 us
    all_gather x1, blocking collectives, step_of_panel(): rows = lax.all_gather(picked, 'prow', axis=0, tiled=True)  26 us
    pallas_call x1, Pallas kernels, by_rows(): pl.pallas_call(kernel, grid=(out[0] // rows,), in_specs=specs, out_specs=...  5.6 us
    pallas_call x1, Pallas kernels, inverse(): pl.pallas_call(inverse_kernel, out_shape=[shape] * 2, scratch_shapes=[plt...  5.32 us
    broadcast_in_dim x2, local copies, waits for them, and re-layouts, exchange(): copies = jnp.broadcast_to(block[None], (len(groups[0]),) + block.shape)  4.23 us
    all_to_all x2, waiting for transfers between devices, exchange(): lax.all_to_all(copies, ('prow', 'pcol'), 0, 0, axis_index_groups=groups)  4.21 us
    ppermute x4, starting transfers between devices, hand_on(): lax.ppermute(home, 'prow', [(i, i + size // 2) for i in range(0, 16, size)])  3.35 us
    pallas_call x1, Pallas kernels, solve(): pl.pallas_call(kernel, in_specs=[pl.BlockSpec(memory_space=pltpu.SMEM)] +...  2.45 us
  transfers between devices with their start and end apart: 6, of which 1 were waited for; matrix products, arithmetic and copies ran while one was open for 5% of the time, Pallas kernels for 11%

commit v1 on v0

--- a/solution.py
+++ b/solution.py
@@ -144,8 +144,10 @@
             v_ref[...] = (-jnp.concatenate([u[i : i + 8] for i in order], axis=0)).astype(BF)
 
 
-def place_solve_kernel(row_ref, a_ref, b_ref, place_ref, got_ref, u_ref, v_ref):
-    finish(row_ref, a_ref, b_ref, placed(place_ref, got_ref).astype(BF), u_ref, v_ref)
+def place_solve_kernel(row_ref, a_ref, b_ref, place_ref, got_ref, u_ref, v_ref, top_ref):
+    top = placed(place_ref, got_ref).astype(BF)
+    top_ref[...] = top
+    finish(row_ref, a_ref, b_ref, top, u_ref, v_ref)
 
 
 def solve_kernel(row_ref, a_ref, b_ref, top_ref, u_ref, v_ref):
@@ -163,7 +165,7 @@
     return tuple(pl.pallas_call(
         kernel,
         in_specs=[pl.BlockSpec(memory_space=pltpu.SMEM)] + [vmem] * (2 + len(rest)),
-        out_shape=[shape] * 2,
+        out_shape=[shape] * (3 if kernel is place_solve_kernel else 2),
         compiler_params=ROOM,
         cost_estimate=pl.CostEstimate(flops=10**9, bytes_accessed=10**7, transcendentals=0),
     )(row, *parts, *rest))
@@ -264,33 +266,29 @@
     near = exchange(l_panel_t, far_groups()).reshape(16 * k, local_rows)
     home = slab[:n]
     got = hand_on(home, 16)
-    got, l_top = lax.optimization_barrier((got, l_top))
+    picked, place, dest, most = picks(jnp.int32(0))
+    rows = lax.all_gather(picked, "prow", axis=0, tiled=True)
+    near, got, rows, l_top = lax.optimization_barrier((near, got, rows, l_top))
+    panel = exchange(near, next_groups()).reshape(n, local_rows)
     home = jnp.where(row == 0, home, got)
     got = hand_on(home, 8)
     parts = inverse(l_top)
-    picked, place, dest, most = picks(jnp.int32(0))
-    near, got, picked, parts = lax.optimization_barrier((near, got, picked, parts))
+    got, parts = lax.optimization_barrier((got, parts))
     home = jnp.where(row % 8 == 0, home, got)
     got = hand_on(home, 4)
-    panel = exchange(near, next_groups()).reshape(n, local_rows)
-    rows = lax.all_gather(picked, "prow", axis=0, tiled=True)
-    got, rows = lax.optimization_barrier((got, rows))
+    u, v, top = solve(place_solve_kernel, r, parts, place, rows)
+    got, u = lax.optimization_barrier((got, u))
     home = jnp.where(row % 4 == 0, home, got)
     sent = hand_on(home, 2)
-    u, v = solve(place_solve_kernel, r, parts, place, rows)
-
-    def in_rounds(_):
-        def step(state):
-            base, top = state
-            picked, place, _, _ = picks(base)
-            rows = lax.all_gather(picked, "prow", axis=0, tiled=True)
-            top = pl.pallas_call(add_kernel, out_shape=jax.ShapeDtypeStruct((n, w), BF))(top, place, rows)
-            return base + CAP, top
-
-        _, top = lax.while_loop(lambda s: s[0] < most[0], step, (jnp.int32(0), jnp.zeros((n, w), BF)))
-        return False, *solve(solve_kernel, r, parts, top)
-
-    _, u, v = lax.while_loop(lambda s: s[0], in_rounds, (most[0] > CAP, u, v))
+
+    def further(state):
+        base, top, _, _ = state
+        picked, place, _, _ = picks(base)
+        rows = lax.all_gather(picked, "prow", axis=0, tiled=True)
+        top = pl.pallas_call(add_kernel, out_shape=jax.ShapeDtypeStruct((n, w), BF))(top, place, rows)
+        return base + CAP, top, *solve(solve_kernel, r, parts, top)
+
+    _, _, u, v = lax.while_loop(lambda s: s[0] < most[0], further, (jnp.int32(CAP), top, u, v))
     flops = 4 * local_rows * n * w
     args = (r, (panel, 1), u, v, dest, home, sent, (slab, 0))
     return by_rows(update_kernel, 512, slab.shape, args, flops, [pltpu.VMEM((2 * n, w + 128), BF)])

time: 85.6 us -> 93.8 us (1.096)
  starting transfers between devices: 32.8 us -> 37.8 us
  other arithmetic: 0.22 us -> 3 us
  Pallas kernels: 15.2 us -> 17.4 us
  blocking collectives: 26 us -> 23.9 us
  waiting for transfers between devices: 4.23 us -> 5.92 us
  local copies, waits for them, and re-layouts: 5.41 us -> 4.27 us
    all_to_all x2, starting transfers between devices: 29.4 us -> 33.8 us  [exchange(): lax.all_to_all(copies, ('prow', 'pcol'), 0, 0, axis_index_groups=groups)]
    all_gather x1, blocking collectives: 26 us -> 23.9 us  [step_of_panel(): rows = lax.all_gather(picked, 'prow', axis=0, tiled=True)]
    ppermute x4, waiting for transfers between devices: 0.01 us -> 1.69 us  [hand_on(): lax.ppermute(home, 'prow', [(i, i + size // 2) for i in range(0, 16, size)])]
    pallas_call x1, Pallas kernels: 2.45 us -> 3.81 us  [solve(): pl.pallas_call(kernel, in_specs=[pl.BlockSpec(memory_space=pltpu.SMEM)] +...]
    select_n x1, other arithmetic: 0.05 us -> 1.07 us  [step_of_panel(): home = jnp.where(row == 0, home, got)]
    broadcast_in_dim x2, local copies, waits for them, and re-layouts: 4.23 us -> 3.23 us  [exchange(): copies = jnp.broadcast_to(block[None], (len(groups[0]),) + block.shape)]
    select_n x1, other arithmetic: 0.05 us -> 1.05 us  [step_of_panel(): home = jnp.where(row % 4 == 0, home, got)]
  transfers between devices with their start and end apart: 6 -> 6, of which waited for: 1 -> 2; matrix products, arithmetic and copies ran while one was open for 5% -> 4% of each run, Pallas kernels for 11% -> 13%
where the time goes in v1:
time: 93.8 us; the launch traced here: 93.1 us
  starting transfers between devices  37.8 us (40%)
  blocking collectives  23.9 us (25%)
  Pallas kernels  17.4 us (19%)
  waiting for transfers between devices  5.92 us (6%)
  local copies, waits for them, and re-layouts  4.27 us (5%)
  other arithmetic  3 us (3%)
    all_to_all x2, starting transfers between devices, exchange(): lax.all_to_all(copies, ('prow', 'pcol'), 0, 0, axis_index_groups=groups)  33.8 us
    all_gather x1, blocking collectives, step_of_panel(): rows = lax.all_gather(picked, 'prow', axis=0, tiled=True)  23.9 us
    pallas_call x1, Pallas kernels, by_rows(): pl.pallas_call(kernel, grid=(out[0] // rows,), in_specs=specs, out_specs=...  5.59 us
    pallas_call x1, Pallas kernels, inverse(): pl.pallas_call(inverse_kernel, out_shape=[shape] * 2, scratch_shapes=[plt...  5.28 us
    all_to_all x2, waiting for transfers between devices, exchange(): lax.all_to_all(copies, ('prow', 'pcol'), 0, 0, axis_index_groups=groups)  4.24 us
    ppermute x4, starting transfers between devices, hand_on(): lax.ppermute(home, 'prow', [(i, i + size // 2) for i in range(0, 16, size)])  4.07 us
    pallas_call x1, Pallas kernels, solve(): pl.pallas_call(kernel, in_specs=[pl.BlockSpec(memory_space=pltpu.SMEM)] +...  3.81 us
    broadcast_in_dim x2, local copies, waits for them, and re-layouts, exchange(): copies = jnp.broadcast_to(block[None], (len(groups[0]),) + block.shape)  3.23 us
  transfers between devices with their start and end apart: 6, of which 2 were waited for; matrix products, arithmetic and copies ran while one was open for 4% of the time, Pallas kernels for 13%

profile of v1, /device:TPU:1, one launch (start us, length us, event | category | flops | bytes accessed | tf_op | source)
XLA Modules:
  0.0 93.1 jit_solution(17316684204080047969)
XLA Ops:
  0.0 0.0 copy-start.3
  0.0 1.6 %broadcast_in_dim.8 = bf16[16,8,2048]{2,1,0:T(8,128)(2,1)} broadcast(bf16[8,2048]{1,0:T(8,128)(2,1)} %param.9), dimensions={1,2} | broadcast | bytes 557056 | tf_op jit(solution)/shard_map/broadcast_in_dim | solution.py:248
  1.6 23.4 %all-to-all-start = ((bf16[16,8,2048]{2,1,0:T(8,128)(2,1)}), bf16[16,8,2048]{2,1,0:T(8,128)(2,1)S(1)}, u32[]{:S(2)}, u32[]{:S(2)}) async-start(bf16[16,8,2048]{2,1,0:T(8,128)(2,1)} %broadcast_in_dim.8), calls=%async_computation | async-start | bytes 1048576 | tf_op jit(solution)/shard_map/all_to_all | solution.py:249
  25.0 1.0 %slice.3 = bf16[512,384]{1,0:T(8,128)(2,1)S(1)} slice(bf16[2048,384]{1,0:T(8,128)(2,1)} %slab_ref.3), slice={[0:512], [0:384]} | slice | bytes 786432 | tf_op jit(solution)/shard_map/slice | solution.py:267
  26.0 0.7 collective-permute-start
  26.7 0.1 pad_add_fusion.1.where_ref
  26.8 0.0 copy-done.3
  26.8 2.7 %shard_map.46 = (bf16[80,384]{1,0:T(8,128)(2,1)S(1)}, s32[512,1]{1,0:T(8,128)S(1)}, s32[1,512]{1,0:T(1,128)S(1)}, s32[1]{0:T(128)}) custom-call(s32[2]{0:T(128)S(1)} %pad_add_fusion.1.where_ref, s32[1,512]{1,0:T(1,128)S(1)} %bitcast.17, bf16[2048,384]{1,0:T(8,128)(2,1)} %slab_ref.3), custom_call_target="tpu_custom_call" | custom-call | flops 2000000000 | bytes 1572864 | tf_op jit(solution)/shard_map/pallas_call | solution.py:60
  29.5 0.0 copy-start.1
  29.5 23.9 %all_gather.6.got_ref = bf16[1280,384]{1,0:T(8,128)(2,1)S(1)} all-gather(bf16[80,384]{1,0:T(8,128)(2,1)S(1)} %get-tuple-element.84), channel_id=1, replica_groups=mesh['prow'=16,'pcol'=64] {'prow'}, dimensions={0}, use_global_device_ids=true | all-gather | bytes 1044480 | tf_op jit(solution)/shard_map/all_gather | solution.py:270
  53.5 0.0 collective-permute-done
  53.5 0.0 all-to-all-done
  53.5 1.1 %broadcast_select_fusion.2 = bf16[512,384]{1,0:T(8,128)(2,1)S(1)} fusion(bf16[512,384]{1,0:T(8,128)(2,1)S(1)} %collective-permute-done, pred[]{:T(512)S(6)} %eq.12, bf16[2048,384]{1,0:T(8,128)(2,1)} %slab_ref.3), kind=kLoop, calls=%fused_computation.3 | loop fusion | flops 196608 | bytes 1179649 | tf_op jit(solution)/shard_map/jit(_where)/select_n | solution.py:273
  54.6 0.7 collective-permute-start.1
  55.3 0.0 copy-done.1
  55.3 5.3 %shard_map.47 = (bf16[512,512]{1,0:T(8,128)(2,1)}, bf16[512,512]{1,0:T(8,128)(2,1)}) custom-call(bf16[512,512]{1,0:T(8,128)(2,1)S(1)} %copy-done.1), custom_call_target="tpu_custom_call" | custom-call | flops 2000000000 | bytes 2097152 | tf_op jit(solution)/shard_map/pallas_call | solution.py:122
  60.6 0.0 collective-permute-done.1
  60.6 0.8 broadcast_select_fusion.1
  61.4 1.4 %collective-permute-start.2 = (bf16[512,384]{1,0:T(8,128)(2,1)}, bf16[512,384]{1,0:T(8,128)(2,1)}, u32[]{:S(2)}, u32[]{:S(2)}) collective-permute-start(bf16[512,384]{1,0:T(8,128)(2,1)} %broadcast_select_fusion.1), channel_id=1, source_target_pairs={{0,128},{256,384},{512,640},{768,896},{1,129},{257,385},{513,641},... | collective-permute-start | bytes 1179656 | tf_op jit(solution)/shard_map/ppermute | solution.py:253
  62.8 1.6 %broadcast_in_dim.20 = bf16[4,128,2048]{2,1,0:T(8,128)(2,1)} broadcast(bf16[128,2048]{1,0:T(8,128)(2,1)S(1)} %bitcast.16), dimensions={1,2} | broadcast | bytes 2621440 | tf_op jit(solution)/shard_map/broadcast_in_dim | solution.py:248
  64.4 10.4 %all-to-all-start.1 = ((bf16[4,128,2048]{2,1,0:T(8,128)(2,1)}), bf16[4,128,2048]{2,1,0:T(8,128)(2,1)S(1)}, u32[]{:S(2)}, u32[]{:S(2)}) async-start(bf16[4,128,2048]{2,1,0:T(8,128)(2,1)} %broadcast_in_dim.20), calls=%async_computation.1 | async-start | bytes 4194304 | tf_op jit(solution)/shard_map/all_to_all | solution.py:249
  74.8 3.8 %shard_map.48 = (bf16[512,384]{1,0:T(8,128)(2,1)}, bf16[512,384]{1,0:T(8,128)(2,1)}, bf16[512,384]{1,0:T(8,128)(2,1)}) custom-call(s32[1]{0:T(128)} %bitcast.4.row_ref, bf16[512,512]{1,0:T(8,128)(2,1)} %get-tuple-element.207.a_ref, bf16[512,512]{1,0:T(8,128)(2,1)} %get-tuple-element.208.b_ref, s32[512,1]{1,0:T(8,128)S(1)} %get-tuple-element.92.place_ref, ...), custom_call_target="tpu_custom_call" | custom-call | flops 1000000000 | bytes 10000000 | tf_op jit(solution)/shard_map/pallas_call | solution.py:165
  78.6 0.0 collective-permute-done.2
  78.6 1.0 %broadcast_select_fusion.own_ref = bf16[512,384]{1,0:T(8,128)(2,1)S(1)} fusion(bf16[512,384]{1,0:T(8,128)(2,1)} %broadcast_select_fusion.1, bf16[512,384]{1,0:T(8,128)(2,1)} %collective-permute-done.2, pred[]{:T(512)S(6)} %eq.14), kind=kLoop, calls=%fused_computation.1 | loop fusion | flops 196608 | bytes 1179649 | tf_op jit(solution)/shard_map/jit(_where)/select_n | solution.py:281
  79.6 1.3 %collective-permute-start.3 = (bf16[512,384]{1,0:T(8,128)(2,1)S(1)}, bf16[512,384]{1,0:T(8,128)(2,1)S(1)}, u32[]{:S(2)}, u32[]{:S(2)}) collective-permute-start(bf16[512,384]{1,0:T(8,128)(2,1)S(1)} %broadcast_select_fusion.own_ref), channel_id=1, source_target_pairs={{0,64},{128,192},{256,320},{384,448},{512,576},{640,704},{768,832}... | collective-permute-start | bytes 1179656 | tf_op jit(solution)/shard_map/ppermute | solution.py:253
  80.9 0.6 while.14
  81.6 1.7 %collective-permute-done.3.sent_ref = bf16[512,384]{1,0:T(8,128)(2,1)S(1)} collective-permute-done((bf16[512,384]{1,0:T(8,128)(2,1)S(1)}, bf16[512,384]{1,0:T(8,128)(2,1)S(1)}, u32[]{:S(2)}, u32[]{:S(2)}) %collective-permute-start.3) | collective-permute-done | bytes 393248 | tf_op jit(solution)/shard_map/ppermute | solution.py:253
  83.3 4.2 %all-to-all-done.1 = bf16[4,128,2048]{2,1,0:T(8,128)(2,1)S(1)} async-done(((bf16[4,128,2048]{2,1,0:T(8,128)(2,1)}), bf16[4,128,2048]{2,1,0:T(8,128)(2,1)S(1)}, u32[]{:S(2)}, u32[]{:S(2)}) %all-to-all-start.1) | async-done | bytes 2097184 | tf_op jit(solution)/shard_map/all_to_all | solution.py:249
  87.5 5.6 %shard_map.49 = bf16[2048,384]{1,0:T(8,128)(2,1)} custom-call(s32[1]{0:T(128)} %bitcast.4.row_ref, bf16[512,2048]{1,0:T(8,128)(2,1)S(1)} %bitcast.15, bf16[512,384]{1,0:T(8,128)(2,1)} %get-tuple-element.100.u_ref, bf16[512,384]{1,0:T(8,128)(2,1)} %get-tuple-element.101.v_ref, s32[1,512]{1,0:T(1,128)S(1)} %get-tuple-element.102.dest_ref, ...), custom_call_target="tpu_custom_call" | custom-call | flops 1610612736 | bytes 6291456 | tf_op jit(solution)/shard_map/pallas_call | solution.py:215
Async XLA Ops:
  0.0 26.8 %copy-start.3 = (s32[512]{0:T(512)S(1)}, s32[512]{0:T(512)}, u32[]{:S(2)}) copy-start(s32[512]{0:T(512)} %param.7) | copy-start | bytes 6148
  1.6 51.9 %all-to-all-start = ((bf16[16,8,2048]{2,1,0:T(8,128)(2,1)}), bf16[16,8,2048]{2,1,0:T(8,128)(2,1)S(1)}, u32[]{:S(2)}, u32[]{:S(2)}) async-start(bf16[16,8,2048]{2,1,0:T(8,128)(2,1)} %broadcast_in_dim.8), calls=%async_computation | async-start | bytes 1048576 | tf_op jit(solution)/shard_map/all_to_all | solution.py:249
  26.0 27.5 %collective-permute-start = (bf16[512,384]{1,0:T(8,128)(2,1)S(1)}, bf16[512,384]{1,0:T(8,128)(2,1)S(1)}, u32[]{:S(2)}, u32[]{:S(2)}) collective-permute-start(bf16[512,384]{1,0:T(8,128)(2,1)S(1)} %slice.3), channel_id=1, source_target_pairs={{0,512},{1,513},{2,514},{3,515},{4,516},{5,517},{6,518},{7,519},{8... | collective-permute-start | bytes 1179656 | tf_op jit(solution)/shard_map/ppermute | solution.py:253
  29.5 25.7 %copy-start.1 = (bf16[512,512]{1,0:T(8,128)(2,1)S(1)}, bf16[512,512]{1,0:T(8,128)(2,1)}, u32[]{:S(2)}) copy-start(bf16[512,512]{1,0:T(8,128)(2,1)} %l_ref) | copy-start | bytes 1572868
  54.6 6.0 %collective-permute-start.1 = (bf16[512,384]{1,0:T(8,128)(2,1)S(1)}, bf16[512,384]{1,0:T(8,128)(2,1)S(1)}, u32[]{:S(2)}, u32[]{:S(2)}) collective-permute-start(bf16[512,384]{1,0:T(8,128)(2,1)S(1)} %broadcast_select_fusion.2), channel_id=1, source_target_pairs={{0,256},{512,768},{1,257},{513,769},{2,258},{514,770},{3,259},{515... | collective-permute-start | bytes 1179656 | tf_op jit(solution)/shard_map/ppermute | solution.py:253
  61.4 17.2 %collective-permute-start.2 = (bf16[512,384]{1,0:T(8,128)(2,1)}, bf16[512,384]{1,0:T(8,128)(2,1)}, u32[]{:S(2)}, u32[]{:S(2)}) collective-permute-start(bf16[512,384]{1,0:T(8,128)(2,1)} %broadcast_select_fusion.1), channel_id=1, source_target_pairs={{0,128},{256,384},{512,640},{768,896},{1,129},{257,385},{513,641},... | collective-permute-start | bytes 1179656 | tf_op jit(solution)/shard_map/ppermute | solution.py:253
  64.4 23.1 %all-to-all-start.1 = ((bf16[4,128,2048]{2,1,0:T(8,128)(2,1)}), bf16[4,128,2048]{2,1,0:T(8,128)(2,1)S(1)}, u32[]{:S(2)}, u32[]{:S(2)}) async-start(bf16[4,128,2048]{2,1,0:T(8,128)(2,1)} %broadcast_in_dim.20), calls=%async_computation.1 | async-start | bytes 4194304 | tf_op jit(solution)/shard_map/all_to_all | solution.py:249
  79.6 3.6 %collective-permute-start.3 = (bf16[512,384]{1,0:T(8,128)(2,1)S(1)}, bf16[512,384]{1,0:T(8,128)(2,1)S(1)}, u32[]{:S(2)}, u32[]{:S(2)}) collective-permute-start(bf16[512,384]{1,0:T(8,128)(2,1)S(1)} %broadcast_select_fusion.own_ref), channel_id=1, source_target_pairs={{0,64},{128,192},{256,320},{384,448},{512,576},{640,704},{768,832}... | collective-permute-start | bytes 1179656 | tf_op jit(solution)/shard_map/ppermute | solution.py:253

commit v2 on v1

--- a/solution.py
+++ b/solution.py
@@ -266,20 +266,20 @@
     near = exchange(l_panel_t, far_groups()).reshape(16 * k, local_rows)
     home = slab[:n]
     got = hand_on(home, 16)
-    picked, place, dest, most = picks(jnp.int32(0))
-    rows = lax.all_gather(picked, "prow", axis=0, tiled=True)
-    near, got, rows, l_top = lax.optimization_barrier((near, got, rows, l_top))
-    panel = exchange(near, next_groups()).reshape(n, local_rows)
+    got, l_top = lax.optimization_barrier((got, l_top))
     home = jnp.where(row == 0, home, got)
     got = hand_on(home, 8)
     parts = inverse(l_top)
-    got, parts = lax.optimization_barrier((got, parts))
+    picked, place, dest, most = picks(jnp.int32(0))
+    near, got, picked, parts = lax.optimization_barrier((near, got, picked, parts))
     home = jnp.where(row % 8 == 0, home, got)
     got = hand_on(home, 4)
-    u, v, top = solve(place_solve_kernel, r, parts, place, rows)
-    got, u = lax.optimization_barrier((got, u))
+    panel = exchange(near, next_groups()).reshape(n, local_rows)
+    rows = lax.all_gather(picked, "prow", axis=0, tiled=True)
+    got, rows = lax.optimization_barrier((got, rows))
     home = jnp.where(row % 4 == 0, home, got)
     sent = hand_on(home, 2)
+    u, v, top = solve(place_solve_kernel, r, parts, place, rows)
 
     def further(state):
         base, top, _, _ = state

time: 93.8 us -> 87.8 us (0.936)
  starting transfers between devices: 37.8 us -> 34.2 us
  Pallas kernels: 17.4 us -> 15.3 us
  blocking collectives: 23.9 us -> 25.9 us
  waiting for transfers between devices: 5.92 us -> 4.03 us
    all_to_all x2, starting transfers between devices: 33.8 us -> 29.4 us  [exchange(): lax.all_to_all(copies, ('prow', 'pcol'), 0, 0, axis_index_groups=groups)]
    all_gather x1, blocking collectives: 23.9 us -> 25.9 us  [step_of_panel(): rows = lax.all_gather(picked, 'prow', axis=0, tiled=True)]
    ppermute x4, waiting for transfers between devices: 1.69 us -> 0.01 us  [hand_on(): lax.ppermute(home, 'prow', [(i, i + size // 2) for i in range(0, 16, size)])]
    pallas_call x1, Pallas kernels: 3.81 us -> 2.46 us  [solve(): pl.pallas_call(kernel, in_specs=[pl.BlockSpec(memory_space=pltpu.SMEM)] +...]
    select_n x1, other arithmetic: 1.07 us -> 0.05 us  [step_of_panel(): home = jnp.where(row == 0, home, got)]
  transfers between devices with their start and end apart: 6 -> 6, of which waited for: 2 -> 1; matrix products, arithmetic and copies ran while one was open for 4% -> 5% of each run, Pallas kernels for 13% -> 11%
where the time goes in v2:
time: 87.8 us; the launch traced here: 86.9 us
  starting transfers between devices  34.2 us (39%)
  blocking collectives  25.9 us (29%)
  Pallas kernels  15.3 us (17%)
  local copies, waits for them, and re-layouts  4.39 us (5%)
  waiting for transfers between devices  4.03 us (5%)
  other arithmetic  2.24 us (3%)
    all_to_all x2, starting transfers between devices, exchange(): lax.all_to_all(copies, ('prow', 'pcol'), 0, 0, axis_index_groups=groups)  29.4 us
    all_gather x1, blocking collectives, step_of_panel(): rows = lax.all_gather(picked, 'prow', axis=0, tiled=True)  25.9 us
    pallas_call x1, Pallas kernels, by_rows(): pl.pallas_call(kernel, grid=(out[0] // rows,), in_specs=specs, out_specs=...  5.62 us
    pallas_call x1, Pallas kernels, inverse(): pl.pallas_call(inverse_kernel, out_shape=[shape] * 2, scratch_shapes=[plt...  5.32 us
    ppermute x4, starting transfers between devices, hand_on(): lax.ppermute(home, 'prow', [(i, i + size // 2) for i in range(0, 16, size)])  4.81 us
    all_to_all x2, waiting for transfers between devices, exchange(): lax.all_to_all(copies, ('prow', 'pcol'), 0, 0, axis_index_groups=groups)  4.02 us
    broadcast_in_dim x2, local copies, waits for them, and re-layouts, exchange(): copies = jnp.broadcast_to(block[None], (len(groups[0]),) + block.shape)  3.21 us
    pallas_call x1, Pallas kernels, solve(): pl.pallas_call(kernel, in_specs=[pl.BlockSpec(memory_space=pltpu.SMEM)] +...  2.46 us
  transfers between devices with their start and end apart: 6, of which 1 were waited for; matrix products, arithmetic and copies ran while one was open for 5% of the time, Pallas kernels for 11%

profile of v2, /device:TPU:1, one launch (start us, length us, event | category | flops | bytes accessed | tf_op | source)
XLA Modules:
  0.0 86.9 jit_solution(4080888125458204329)
XLA Ops:
  0.0 0.0 copy-start.2
  0.0 1.2 %slice.3 = bf16[512,384]{1,0:T(8,128)(2,1)S(1)} slice(bf16[2048,384]{1,0:T(8,128)(2,1)} %slab_ref.3), slice={[0:512], [0:384]} | slice | bytes 786432 | tf_op jit(solution)/shard_map/slice | solution.py:267
  1.2 0.0 copy-start.3
  1.2 0.7 collective-permute-start
  1.9 1.6 %broadcast_in_dim.8 = bf16[16,8,2048]{2,1,0:T(8,128)(2,1)} broadcast(bf16[8,2048]{1,0:T(8,128)(2,1)} %param.9), dimensions={1,2} | broadcast | bytes 557056 | tf_op jit(solution)/shard_map/broadcast_in_dim | solution.py:248
  3.5 23.4 %all-to-all-start = ((bf16[16,8,2048]{2,1,0:T(8,128)(2,1)}), bf16[16,8,2048]{2,1,0:T(8,128)(2,1)S(1)}, u32[]{:S(2)}, u32[]{:S(2)}) async-start(bf16[16,8,2048]{2,1,0:T(8,128)(2,1)} %broadcast_in_dim.8), calls=%async_computation | async-start | bytes 1048576 | tf_op jit(solution)/shard_map/all_to_all | solution.py:249
  26.8 0.0 collective-permute-done
  26.9 0.0 copy-done.2
  26.9 0.1 broadcast_select_fusion.2
  26.9 1.4 %collective-permute-start.1 = (bf16[512,384]{1,0:T(8,128)(2,1)S(1)}, bf16[512,384]{1,0:T(8,128)(2,1)}, u32[]{:S(2)}, u32[]{:S(2)}) collective-permute-start(bf16[512,384]{1,0:T(8,128)(2,1)S(1)} %broadcast_select_fusion.2), channel_id=1, source_target_pairs={{0,256},{512,768},{1,257},{513,769},{2,258},{514,770},{3,259},{515... | collective-permute-start | bytes 1179656 | tf_op jit(solution)/shard_map/ppermute | solution.py:253
  28.3 0.1 pad_add_fusion.1.where_ref
  28.4 0.0 copy-done.3
  28.4 0.0 copy-start.1
  28.4 1.9 %shard_map.46 = (bf16[80,384]{1,0:T(8,128)(2,1)S(1)}, s32[512,1]{1,0:T(8,128)S(1)}, s32[1,512]{1,0:T(1,128)S(1)}, s32[1]{0:T(128)}) custom-call(s32[2]{0:T(128)S(1)} %pad_add_fusion.1.where_ref, s32[1,512]{1,0:T(1,128)S(1)} %bitcast.17, bf16[2048,384]{1,0:T(8,128)(2,1)S(1)} %copy-done.2), custom_call_target="tpu_custom_call" | custom-call | flops 2000000000 | bytes 1572864 | tf_op jit(solution)/shard_map/pallas_call | solution.py:60
  30.3 0.0 copy-done.1
  30.3 5.3 %shard_map.47 = (bf16[512,512]{1,0:T(8,128)(2,1)}, bf16[512,512]{1,0:T(8,128)(2,1)}) custom-call(bf16[512,512]{1,0:T(8,128)(2,1)S(1)} %copy-done.1), custom_call_target="tpu_custom_call" | custom-call | flops 2000000000 | bytes 2097152 | tf_op jit(solution)/shard_map/pallas_call | solution.py:122
  35.6 0.0 collective-permute-done.1
  35.6 4.0 %all-to-all-done = bf16[16,8,2048]{2,1,0:T(8,128)(2,1)S(1)} async-done(((bf16[16,8,2048]{2,1,0:T(8,128)(2,1)}), bf16[16,8,2048]{2,1,0:T(8,128)(2,1)S(1)}, u32[]{:S(2)}, u32[]{:S(2)}) %all-to-all-start) | async-done | bytes 524320 | tf_op jit(solution)/shard_map/all_to_all | solution.py:249
  39.6 1.1 %broadcast_select_fusion.1 = bf16[512,384]{1,0:T(8,128)(2,1)S(1)} fusion(bf16[512,384]{1,0:T(8,128)(2,1)S(1)} %broadcast_select_fusion.2, bf16[512,384]{1,0:T(8,128)(2,1)} %collective-permute-done.1, pred[]{:T(512)S(6)} %eq.13), kind=kLoop, calls=%fused_computation.2 | loop fusion | flops 196608 | bytes 1179649 | tf_op jit(solution)/shard_map/jit(_where)/select_n | solution.py:275
  40.7 1.4 %collective-permute-start.2 = (bf16[512,384]{1,0:T(8,128)(2,1)S(1)}, bf16[512,384]{1,0:T(8,128)(2,1)}, u32[]{:S(2)}, u32[]{:S(2)}) collective-permute-start(bf16[512,384]{1,0:T(8,128)(2,1)S(1)} %broadcast_select_fusion.1), channel_id=1, source_target_pairs={{0,128},{256,384},{512,640},{768,896},{1,129},{257,385},{513,641},... | collective-permute-start | bytes 1179656 | tf_op jit(solution)/shard_map/ppermute | solution.py:253
  42.1 1.6 %broadcast_in_dim.20 = bf16[4,128,2048]{2,1,0:T(8,128)(2,1)} broadcast(bf16[128,2048]{1,0:T(8,128)(2,1)S(1)} %bitcast.16), dimensions={1,2} | broadcast | bytes 2621440 | tf_op jit(solution)/shard_map/broadcast_in_dim | solution.py:248
  43.7 6.1 %all-to-all-start.1 = ((bf16[4,128,2048]{2,1,0:T(8,128)(2,1)}), bf16[4,128,2048]{2,1,0:T(8,128)(2,1)S(1)}, u32[]{:S(2)}, u32[]{:S(2)}) async-start(bf16[4,128,2048]{2,1,0:T(8,128)(2,1)} %broadcast_in_dim.20), calls=%async_computation.1 | async-start | bytes 4194304 | tf_op jit(solution)/shard_map/all_to_all | solution.py:249
  49.8 0.0 copy-start.4
  49.8 0.0 copy-start.5
  49.8 25.9 %all_gather.6.got_ref = bf16[1280,384]{1,0:T(8,128)(2,1)S(1)} all-gather(bf16[80,384]{1,0:T(8,128)(2,1)S(1)} %get-tuple-element.94), channel_id=1, replica_groups=mesh['prow'=16,'pcol'=64] {'prow'}, dimensions={0}, use_global_device_ids=true | all-gather | bytes 1044480 | tf_op jit(solution)/shard_map/all_gather | solution.py:278
  75.7 0.0 collective-permute-done.2
  75.7 1.1 %broadcast_select_fusion.own_ref = bf16[512,384]{1,0:T(8,128)(2,1)S(1)} fusion(bf16[512,384]{1,0:T(8,128)(2,1)S(1)} %broadcast_select_fusion.1, bf16[512,384]{1,0:T(8,128)(2,1)} %collective-permute-done.2, pred[]{:T(512)S(6)} %eq.14), kind=kLoop, calls=%fused_computation.1 | loop fusion | flops 196608 | bytes 1179649 | tf_op jit(solution)/shard_map/jit(_where)/select_n | solution.py:280
  76.8 1.3 %collective-permute-start.3 = (bf16[512,384]{1,0:T(8,128)(2,1)S(1)}, bf16[512,384]{1,0:T(8,128)(2,1)S(1)}, u32[]{:S(2)}, u32[]{:S(2)}) collective-permute-start(bf16[512,384]{1,0:T(8,128)(2,1)S(1)} %broadcast_select_fusion.own_ref), channel_id=1, source_target_pairs={{0,64},{128,192},{256,320},{384,448},{512,576},{640,704},{768,832}... | collective-permute-start | bytes 1179656 | tf_op jit(solution)/shard_map/ppermute | solution.py:253
  78.1 0.0 copy-done.4
  78.1 0.0 copy-done.5
  78.1 2.5 %shard_map.48 = (bf16[512,384]{1,0:T(8,128)(2,1)}, bf16[512,384]{1,0:T(8,128)(2,1)}, bf16[512,384]{1,0:T(8,128)(2,1)S(1)}) custom-call(s32[1]{0:T(128)} %bitcast.4.row_ref, bf16[512,512]{1,0:T(8,128)(2,1)S(1)} %copy-done.4, bf16[512,512]{1,0:T(8,128)(2,1)S(1)} %copy-done.5, s32[512,1]{1,0:T(8,128)S(1)} %get-tuple-element.92.place_ref, ...), custom_call_target="tpu_custom_call" | custom-call | flops 1000000000 | bytes 10000000 | tf_op jit(solution)/shard_map/pallas_call | solution.py:165
  80.6 0.6 while.14
  81.2 0.0 collective-permute-done.3.sent_ref
  81.2 0.0 all-to-all-done.1
  81.2 5.6 %shard_map.49 = bf16[2048,384]{1,0:T(8,128)(2,1)} custom-call(s32[1]{0:T(128)} %bitcast.4.row_ref, bf16[512,2048]{1,0:T(8,128)(2,1)S(1)} %bitcast.15, bf16[512,384]{1,0:T(8,128)(2,1)} %get-tuple-element.100.u_ref, bf16[512,384]{1,0:T(8,128)(2,1)} %get-tuple-element.101.v_ref, s32[1,512]{1,0:T(1,128)S(1)} %get-tuple-element.102.dest_ref, ...), custom_call_target="tpu_custom_call" | custom-call | flops 1610612736 | bytes 6291456 | tf_op jit(solution)/shard_map/pallas_call | solution.py:215
Async XLA Ops:
  0.0 26.9 %copy-start.2 = (bf16[2048,384]{1,0:T(8,128)(2,1)S(1)}, bf16[2048,384]{1,0:T(8,128)(2,1)}, u32[]{:S(2)}) copy-start(bf16[2048,384]{1,0:T(8,128)(2,1)} %slab_ref.3) | copy-start | bytes 4718596
  1.2 27.3 %copy-start.3 = (s32[512]{0:T(512)S(1)}, s32[512]{0:T(512)}, u32[]{:S(2)}) copy-start(s32[512]{0:T(512)} %param.7) | copy-start | bytes 6148
  1.2 25.7 %collective-permute-start = (bf16[512,384]{1,0:T(8,128)(2,1)S(1)}, bf16[512,384]{1,0:T(8,128)(2,1)S(1)}, u32[]{:S(2)}, u32[]{:S(2)}) collective-permute-start(bf16[512,384]{1,0:T(8,128)(2,1)S(1)} %slice.3), channel_id=1, source_target_pairs={{0,512},{1,513},{2,514},{3,515},{4,516},{5,517},{6,518},{7,519},{8... | collective-permute-start | bytes 1179656 | tf_op jit(solution)/shard_map/ppermute | solution.py:253
  3.5 36.2 %all-to-all-start = ((bf16[16,8,2048]{2,1,0:T(8,128)(2,1)}), bf16[16,8,2048]{2,1,0:T(8,128)(2,1)S(1)}, u32[]{:S(2)}, u32[]{:S(2)}) async-start(bf16[16,8,2048]{2,1,0:T(8,128)(2,1)} %broadcast_in_dim.8), calls=%async_computation | async-start | bytes 1048576 | tf_op jit(solution)/shard_map/all_to_all | solution.py:249
  26.9 8.7 %collective-permute-start.1 = (bf16[512,384]{1,0:T(8,128)(2,1)S(1)}, bf16[512,384]{1,0:T(8,128)(2,1)}, u32[]{:S(2)}, u32[]{:S(2)}) collective-permute-start(bf16[512,384]{1,0:T(8,128)(2,1)S(1)} %broadcast_select_fusion.2), channel_id=1, source_target_pairs={{0,256},{512,768},{1,257},{513,769},{2,258},{514,770},{3,259},{515... | collective-permute-start | bytes 1179656 | tf_op jit(solution)/shard_map/ppermute | solution.py:253
  28.4 1.9 %copy-start.1 = (bf16[512,512]{1,0:T(8,128)(2,1)S(1)}, bf16[512,512]{1,0:T(8,128)(2,1)}, u32[]{:S(2)}) copy-start(bf16[512,512]{1,0:T(8,128)(2,1)} %l_ref) | copy-start | bytes 1572868
  40.7 35.0 %collective-permute-start.2 = (bf16[512,384]{1,0:T(8,128)(2,1)S(1)}, bf16[512,384]{1,0:T(8,128)(2,1)}, u32[]{:S(2)}, u32[]{:S(2)}) collective-permute-start(bf16[512,384]{1,0:T(8,128)(2,1)S(1)} %broadcast_select_fusion.1), channel_id=1, source_target_pairs={{0,128},{256,384},{512,640},{768,896},{1,129},{257,385},{513,641},... | collective-permute-start | bytes 1179656 | tf_op jit(solution)/shard_map/ppermute | solution.py:253
  43.7 37.5 %all-to-all-start.1 = ((bf16[4,128,2048]{2,1,0:T(8,128)(2,1)}), bf16[4,128,2048]{2,1,0:T(8,128)(2,1)S(1)}, u32[]{:S(2)}, u32[]{:S(2)}) async-start(bf16[4,128,2048]{2,1,0:T(8,128)(2,1)} %broadcast_in_dim.20), calls=%async_computation.1 | async-start | bytes 4194304 | tf_op jit(solution)/shard_map/all_to_all | solution.py:249
  49.8 28.3 %copy-start.4 = (bf16[512,512]{1,0:T(8,128)(2,1)S(1)}, bf16[512,512]{1,0:T(8,128)(2,1)}, u32[]{:S(2)}) copy-start(bf16[512,512]{1,0:T(8,128)(2,1)} %get-tuple-element.207.a_ref) | copy-start | bytes 1572868
  49.8 28.3 %copy-start.5 = (bf16[512,512]{1,0:T(8,128)(2,1)S(1)}, bf16[512,512]{1,0:T(8,128)(2,1)}, u32[]{:S(2)}) copy-start(bf16[512,512]{1,0:T(8,128)(2,1)} %get-tuple-element.208.b_ref) | copy-start | bytes 1572868
  76.8 4.4 %collective-permute-start.3 = (bf16[512,384]{1,0:T(8,128)(2,1)S(1)}, bf16[512,384]{1,0:T(8,128)(2,1)S(1)}, u32[]{:S(2)}, u32[]{:S(2)}) collective-permute-start(bf16[512,384]{1,0:T(8,128)(2,1)S(1)} %broadcast_select_fusion.own_ref), channel_id=1, source_target_pairs={{0,64},{128,192},{256,320},{384,448},{512,576},{640,704},{768,832}... | collective-permute-start | bytes 1179656 | tf_op jit(solution)/shard_map/ppermute | solution.py:253
